TPU v7x, 16 devices: a whole 2x2x2 slice. The times are simulated.
16 devices in a mesh: data: 4 (over z, y), tp: 4 (over x, core).
Axes of the slice: x: 2, y: 2, z: 2, core: 2. Of those that a mesh axis runs over, the one named last changes fastest.
Arguments:
- x: bfloat16 [2048, 49152], P('data', 'tp'), parts along dimension 0
- w: bfloat16 [49152, 12288], P('tp')
Outputs:
- output: bfloat16 [2048, 12288], P('data'), parts along dimension 0
There are 4 independent parts. A program takes and returns all parts, laid end to end along the dimension named above; an argument that names none is the same for every part.
All inputs are finite; a program needn't handle non-finite values.
Results may differ from a plain program's by a relative error of at most 0.0103023.
Values are sent between devices in bfloat16 or wider.
A program may use at most 1.25 GiB of HBM per device.

v0:
```python
import jax
import jax.numpy as jnp
from jax import lax
from jax.sharding import PartitionSpec as P, NamedSharding


def solution(mesh):
    def local(x, w):
        partial_y = jnp.dot(x, w, preferred_element_type=jnp.float32).astype(jnp.bfloat16)
        reduced = lax.psum_scatter(partial_y, "tp", scatter_dimension=0, tiled=True)
        return lax.all_gather(reduced, "tp", axis=0, tiled=True)

    return jax.shard_map(local, mesh=mesh, in_specs=(P("data", "tp"), P("tp", None)), out_specs=P("data", None), check_vma=False)
```

profile of v0, /device:TPU:0, one launch (start us, length us, event | category | flops | bytes accessed | tf_op | source)
XLA Modules:
  0.0 370.6 jit_solution(6539651037717852147)
XLA Ops:
  6.5 0.0 reduce-scatter.2.cloned.1.call-start
  6.5 168.7 %convolution_convert_fusion = bf16[512,12288]{1,0:T(8,128)(2,1)} fusion(bf16[512,12288]{1,0:T(8,128)(2,1)} %param.2, bf16[12288,12288]{1,0:T(8,128)(2,1)} %param.3), kind=kOutput, calls=%fused_computation | convolution fusion | flops 154625114112 | bytes 327155712 | tf_op jit(solution)/shard_map/dot_general | solution.py:9
  175.2 0.0 reduce-scatter.2.cloned.1.call-update
  175.3 0.0 all-gather.2.cloned.1.call-start
  175.3 95.3 %reduce-scatter.2.cloned.1.call-done = bf16[128,12288]{1,0:T(8,128)(2,1)} async-done(((bf16[512,12288]{1,0:T(8,128)(2,1)}), bf16[128,12288]{1,0:T(8,128)(2,1)}) %reduce-scatter.2.cloned.1.call-update) | async-done | bytes 3145744 | tf_op jit(solution)/shard_map/reduce_scatter | solution.py:10
  270.6 0.0 all-gather.2.cloned.1.call-update
  270.7 82.4 %all-gather.2.cloned.1.call-done = bf16[512,12288]{1,0:T(8,128)(2,1)} async-done(((bf16[128,12288]{1,0:T(8,128)(2,1)}), bf16[512,12288]{1,0:T(8,128)(2,1)}) %all-gather.2.cloned.1.call-update) | async-done | bytes 12582928 | tf_op jit(solution)/shard_map/all_gather | solution.py:11
  353.1 10.6 %copy.4 = bf16[512,12288]{1,0:T(8,128)(2,1)} copy(bf16[512,12288]{1,0:T(8,128)(2,1)} %all-gather.2.cloned.1.call-done) | data formatting | bytes 25165824
Async XLA Ops:
  6.5 264.1 %reduce-scatter.2.cloned.1.call-start = ((), (), s32[]{:S(2)}) async-start(), calls=%async_computation.1 | async-start | bytes 15728640 | tf_op jit(solution)/shard_map/reduce_scatter | solution.py:10
  175.3 177.8 %all-gather.2.cloned.1.call-start = ((), (), s32[]{:S(2)}) async-start(), calls=%async_computation.2 | async-start | bytes 15728640 | tf_op jit(solution)/shard_map/all_gather | solution.py:11
Sparse Core Ops, SparseCore 0:
  175.4 95.2 reduce-scatter.1
  272.2 80.8 all-gather.1
where the time goes:
time: 371 us
  waiting for transfers between devices  178 us (48%)
  matrix products  169 us (46%)
  between operations  13.4 us (4%)
  local copies, waits for them, and re-layouts  10.6 us (3%)
    dot_general x1, matrix products, local(): jnp.dot(x, w, preferred_element_type=jnp.float32).astype(jnp.bfloat16)  169 us
    reduce_scatter x1, waiting for transfers between devices, local(): reduced = lax.psum_scatter(partial_y, 'tp', scatter_dimension=0, tiled=True)  95.3 us
    all_gather x1, waiting for transfers between devices, local(): return lax.all_gather(reduced, 'tp', axis=0, tiled=True)  82.4 us
    unnamed x1, local copies, waits for them, and re-layouts  10.6 us
  transfers between devices with their start and end apart: 2, of which 2 were waited for; matrix products, arithmetic and copies ran while one was open for 0% of the time, Pallas kernels for 0%

commit v1 on v0

v1 whole, which is shorter than its diff:
```python
import functools

import jax
import jax.numpy as jnp
from jax import lax
from jax.experimental import pallas as pl
from jax.experimental.pallas import tpu as pltpu
from jax.sharding import PartitionSpec as P

MESH = pl.DeviceIdType.MESH
BF16 = jnp.bfloat16
F32 = jnp.float32
HALF = 256
TILE = 2 * HALF
CHUNKS = 8
SLOTS = CHUNKS
LAG = 3
PIECE = 256


def fused(x, w, y, xv, wv, acc, own, pbuf, precv, sbuf, x_sem, w_sem, p_send, p_recv, s_send, s_recv, y_send, y_recv):
    rows, depth = x.shape
    tiles = w.shape[1] // TILE
    chunk = depth // CHUNKS
    pushes = chunk // HALF
    pieces = rows // PIECE
    me = lax.axis_index("tp")
    core = lax.rem(me, 2)
    partner = me + 1 - 2 * core
    across = lax.rem(me + 2, 4)

    def x_copy(q):
        cols = pl.ds(q * chunk, chunk)
        return pltpu.make_async_copy(x.at[:, cols], xv.at[:, cols], x_sem.at[q])

    def w_copies(t, q):
        deep = pl.ds(q * chunk, chunk)
        return [
            pltpu.make_async_copy(
                w.at[deep, pl.ds(pl.multiple_of(t * TILE + half * HALF, HALF), HALF)],
                wv.at[q, m],
                w_sem.at[q, m],
            )
            for m, half in enumerate((core, 1 - core))
        ]

    def p_copy(v):
        s = lax.rem(v, 2)
        return pltpu.make_async_remote_copy(
            src_ref=pbuf, dst_ref=precv.at[s], send_sem=p_send.at[s], recv_sem=p_recv.at[s],
            device_id={"tp": partner}, device_id_type=MESH,
        )

    def s_copy(v):
        s = lax.rem(v, 4)
        return pltpu.make_async_remote_copy(
            src_ref=sbuf.at[lax.rem(v, 2)], dst_ref=y.at[v + LAG, core], send_sem=s_send.at[s], recv_sem=s_recv.at[s],
            device_id={"tp": across}, device_id_type=MESH,
        )

    def y_copy(v):
        return pltpu.make_async_remote_copy(
            src_ref=y.at[v + LAG, core], dst_ref=y.at[v + LAG, core], send_sem=y_send.at[v], recv_sem=y_recv.at[v],
            device_id={"tp": partner}, device_id_type=MESH,
        )

    def sum_chip(v):
        sbuf[lax.rem(v, 2)] = (own[...] + precv[lax.rem(v, 2)].astype(F32)).astype(BF16)

    def sum_all(v):
        y[v + LAG, core] = (sbuf[lax.rem(v + 4, 2)].astype(F32) + y[v + LAG, core].astype(F32)).astype(BF16)

    def body():
        def pop(parity):
            own[...] = acc[parity, 0]
            pbuf[...] = acc[parity, 1].astype(BF16)

        for q in range(SLOTS - 1):
            x_copy(q).start()
            for c in w_copies(0, q):
                c.start()
        x_copy(CHUNKS - 1).start()

        barrier = pltpu.get_barrier_semaphore()
        for other in (partner, across):
            pl.semaphore_signal(barrier, inc=1, device_id={"tp": other}, device_id_type=MESH)
        pl.semaphore_wait(barrier, 2)

        x_copy(0).wait()
        for c in w_copies(0, 0):
            c.wait()

        def two_tiles(i, carry):
            for parity in range(2):
                t = 2 * i + parity
                for q in range(CHUNKS):
                    if q == CHUNKS - 1:
                        if parity == 0:
                            for c in w_copies(t + 1, 0):
                                c.wait()
                        else:
                            @pl.when(t + 1 < tiles)
                            def _():
                                for c in w_copies(t + 1, 0):
                                    c.wait()
                    else:
                        if parity == 0:
                            @pl.when(t == 0)
                            def _():
                                x_copy(q + 1).wait()
                        for c in w_copies(t, q + 1):
                            c.wait()
                    if q == 0:
                        for c in w_copies(t, CHUNKS - 1):
                            c.start()
                    elif parity == 0:
                        for c in w_copies(t + 1, q - 1):
                            c.start()
                    else:
                        @pl.when(t + 1 < tiles)
                        def _():
                            for c in w_copies(t + 1, q - 1):
                                c.start()
                    if q == 0:
                        @pl.when(t >= LAG)
                        def _():
                            s_copy(t - LAG).wait()
                    if q == 2:
                        @pl.when(t >= LAG)
                        def _():
                            y_copy(t - LAG).start()
                        @pl.when(t >= 1)
                        def _():
                            p_copy(t - 1).start()
                    if q == 4:
                        @pl.when(t >= 1)
                        def _():
                            p_copy(t - 1).wait()
                    if q == 5:
                        @pl.when(t >= 1)
                        def _():
                            s_copy(t - 1).start()

                    for m in range(2):
                        part = jnp.dot(xv[:, pl.ds(q * chunk, chunk)], wv[q, m], preferred_element_type=F32)
                        acc[parity, m] = part if q == 0 else acc[parity, m] + part
                    if q == 0:
                        sum_all(t - LAG)
                    if q == 1:
                        pop(1 - parity)
                    if q == 4:
                        sum_chip(t + 1)
            return carry

        lax.fori_loop(0, tiles // 2, two_tiles, 0)

        last = tiles - 1
        pop(last % 2)
        p_copy(last).start()
        s_copy(last - 2).wait()
        sum_all(last - 2)
        y_copy(last - 2).start()
        p_copy(last).wait()
        sum_chip(last)
        s_copy(last).start()
        for v in (last - 1, last):
            s_copy(v).wait()
            sum_all(v)
            y_copy(v).start()

        def finish(v, carry):
            y_copy(v).wait()
            return carry

        lax.fori_loop(0, tiles, finish, 0)

    body()


def place(y, out, sems):
    tiles = out.shape[1] // TILE
    copies = []
    for t in range(tiles):
        for h in range(2):
            copies.append(
                pltpu.make_async_copy(y.at[t + LAG, h], out.at[:, pl.ds(t * TILE + h * HALF, HALF)], sems.at[2 * t + h])
            )
    for c in copies:
        c.start()
    for c in copies:
        c.wait()


def solution(mesh):
    def local(x, w):
        rows, depth = x.shape
        columns = w.shape[1]
        tiles = columns // TILE
        chunk = depth // CHUNKS
        x = pltpu.with_memory_space_constraint(x, pltpu.HBM)
        w = pltpu.with_memory_space_constraint(w, pltpu.HBM)
        y = pl.pallas_call(
            fused,
            out_shape=pltpu.VMEM((tiles + LAG, 2, rows, HALF), BF16),
            in_specs=[pl.BlockSpec(memory_space=pl.ANY)] * 2,
            out_specs=pl.BlockSpec(memory_space=pltpu.VMEM),
            scratch_shapes=[
                pltpu.VMEM((rows, depth), BF16),
                pltpu.VMEM((SLOTS, 2, chunk, HALF), BF16),
                pltpu.VMEM((2, 2, rows, HALF), F32),
                pltpu.VMEM((rows, HALF), F32),
                pltpu.VMEM((rows, HALF), BF16),
                pltpu.VMEM((2, rows, HALF), BF16),
                pltpu.VMEM((2, rows, HALF), BF16),
                pltpu.SemaphoreType.DMA((CHUNKS,)),
                pltpu.SemaphoreType.DMA((SLOTS, 2)),
                pltpu.SemaphoreType.DMA((2,)),
                pltpu.SemaphoreType.DMA((2,)),
                pltpu.SemaphoreType.DMA((4,)),
                pltpu.SemaphoreType.DMA((4,)),
                pltpu.SemaphoreType.DMA((tiles,)),
                pltpu.SemaphoreType.DMA((tiles,)),
            ],
            compiler_params=pltpu.CompilerParams(
                collective_id=0, has_side_effects=True, vmem_limit_bytes=48 * 2**20
            ),
            name="fused",
        )(x, w)
        return pl.pallas_call(
            place,
            out_shape=jax.ShapeDtypeStruct((rows, columns), BF16),
            in_specs=[pl.BlockSpec(memory_space=pltpu.VMEM)],
            out_specs=pl.BlockSpec(memory_space=pl.ANY),
            scratch_shapes=[pltpu.SemaphoreType.DMA((2 * tiles,))],
            compiler_params=pltpu.CompilerParams(vmem_limit_bytes=16 * 2**20),
            name="place",
        )(y)

    return jax.shard_map(local, mesh=mesh, in_specs=(P("data", "tp"), P("tp", None)), out_specs=P("data", None), check_vma=False)
```

time: 371 us -> 198 us (0.53)
  Pallas kernels: 0 us -> 198 us
  waiting for transfers between devices: 178 us -> 0 us
  matrix products: 169 us -> 0 us
  between operations: 13.4 us -> 0.01 us
  local copies, waits for them, and re-layouts: 10.6 us -> 0 us
    pallas_call x0 -> x2, Pallas kernels: none -> 198 us  [the longest x1 193 us: local(): pl.pallas_call(fused, out_shape=pltpu.VMEM((tiles + LAG, 2, rows, HALF),...]
    dot_general x1 -> x0, matrix products: 169 us -> none  [local(): jnp.dot(x, w, preferred_element_type=jnp.float32).astype(jnp.bfloat16)]
    reduce_scatter x1 -> x0, waiting for transfers between devices: 95.3 us -> none  [local(): reduced = lax.psum_scatter(partial_y, 'tp', scatter_dimension=0, tiled=True)]
    all_gather x1 -> x0, waiting for transfers between devices: 82.4 us -> none  [local(): return lax.all_gather(reduced, 'tp', axis=0, tiled=True)]
    unnamed x1 -> x0, local copies, waits for them, and re-layouts: 10.6 us -> none
  transfers between devices with their start and end apart: 2 -> 0, of which waited for: 2 -> 0; matrix products, arithmetic and copies ran while one was open for 0% -> 0% of each run, Pallas kernels for 0% -> 0%
where the time goes in v1:
time: 198 us
  Pallas kernels  198 us (100%)
    pallas_call x1, Pallas kernels, local(): pl.pallas_call(fused, out_shape=pltpu.VMEM((tiles + LAG, 2, rows, HALF),...  193 us
    pallas_call x1, Pallas kernels, local(): pl.pallas_call(place, out_shape=jax.ShapeDtypeStruct((rows, columns), BF1...  4.94 us

profile of v1, /device:TPU:0, one launch (start us, length us, event | category | flops | bytes accessed | tf_op | source)
XLA Modules:
  0.0 197.8 jit_solution(1941012461233359847)
XLA Ops:
  0.0 192.8 %fused.1.y = bf16[27,2,512,256]{3,2,1,0:T(8,128)(2,1)S(1)} custom-call(bf16[512,12288]{1,0:T(8,128)(2,1)} %x.1, bf16[12288,12288]{1,0:T(8,128)(2,1)} %w.1), custom_call_target="tpu_custom_call" | custom-call | tf_op jit(solution)/shard_map/fused/pallas_call | solution.py:202
  192.8 4.9 %place.1 = bf16[512,12288]{1,0:T(8,128)(2,1)} custom-call(bf16[27,2,512,256]{3,2,1,0:T(8,128)(2,1)S(1)} %fused.1.y), custom_call_target="tpu_custom_call" | custom-call | tf_op jit(solution)/shard_map/place/pallas_call | solution.py:229

commit v2 on v0

v2 whole, which is shorter than its diff:
```python
import jax
import jax.numpy as jnp
from jax import lax
from jax.experimental import pallas as pl
from jax.experimental.pallas import tpu as pltpu
from jax.sharding import PartitionSpec as P

MESH = pl.DeviceIdType.MESH
BF16 = jnp.bfloat16
F32 = jnp.float32
HALF = 256
TILE = 2 * HALF
CHUNKS = 8
PIECE = 128
LAG = 3


def fused(x, w, y, xv, wv, acc, own, pbuf, precv, sbuf, x_sem, w0_sem, w_sem, p_send, p_recv, s_send, s_recv, y_send, y_recv):
    depth = x.shape[1]
    tiles = w.shape[1] // TILE
    chunk = depth // CHUNKS
    pieces = [pl.ds(r, PIECE) for r in range(0, x.shape[0], PIECE)]
    me = lax.axis_index("tp")
    core = lax.rem(me, 2)
    partner = me + 1 - 2 * core
    across = lax.rem(me + 2, 4)

    def columns(t, half):
        return pl.ds(pl.multiple_of(t * TILE + half * HALF, HALF), HALF)

    def own_ref(t):
        return wv.at[lax.rem(t, 2), :, pl.ds(HALF, HALF)]

    def other_ref(t):
        return wv.at[lax.rem(t + 1, 2), :, pl.ds(0, HALF)]

    def own_slab(t):
        return pltpu.make_async_copy(w.at[:, columns(t, core)], own_ref(t), w_sem.at[1, lax.rem(t, 2)])

    def other_slab(t):
        return pltpu.make_async_copy(w.at[:, columns(t, 1 - core)], other_ref(t), w_sem.at[0, lax.rem(t, 2)])

    def x_copy(q):
        cols = pl.ds(pl.multiple_of(q * chunk, chunk), chunk)
        return pltpu.make_async_copy(x.at[:, cols], xv.at[:, cols], x_sem.at[q])

    def first_copies(q):
        deep = pl.ds(pl.multiple_of(q * chunk, chunk), chunk)
        return [
            pltpu.make_async_copy(w.at[deep, columns(0, 1 - core)], wv.at[1, deep, pl.ds(0, HALF)], w0_sem.at[0, q]),
            pltpu.make_async_copy(w.at[deep, columns(0, core)], wv.at[0, deep, pl.ds(HALF, HALF)], w0_sem.at[1, q]),
        ]

    def p_copy(v):
        s = lax.rem(v, 2)
        return pltpu.make_async_remote_copy(
            src_ref=pbuf.at[s], dst_ref=precv.at[s], send_sem=p_send.at[s], recv_sem=p_recv.at[s],
            device_id={"tp": partner}, device_id_type=MESH,
        )

    def s_copy(v):
        s = lax.rem(v, 4)
        return pltpu.make_async_remote_copy(
            src_ref=sbuf.at[s], dst_ref=y.at[v + LAG, core], send_sem=s_send.at[v], recv_sem=s_recv.at[v],
            device_id={"tp": across}, device_id_type=MESH,
        )

    def y_copy(v):
        return pltpu.make_async_remote_copy(
            src_ref=y.at[v + LAG, core], dst_ref=y.at[v + LAG, core], send_sem=y_send.at[v], recv_sem=y_recv.at[v],
            device_id={"tp": partner}, device_id_type=MESH,
        )

    def sum_chip(v):
        for at in pieces:
            sbuf[lax.rem(v, 4), at] = own[at] + precv[lax.rem(v, 2), at]

    def sum_all(v):
        for at in pieces:
            y[v + LAG, core, at] = sbuf[lax.rem(v + 4, 4), at] + y[v + LAG, core, at]

    def product(weights):
        return jnp.dot(xv[...], weights[...], preferred_element_type=F32).astype(BF16)

    for q in range(CHUNKS):
        x_copy(q).start()
        for c in first_copies(q):
            c.start()
    other_slab(1).start()
    own_slab(1).start()

    barrier = pltpu.get_barrier_semaphore()
    for other in (partner, across):
        pl.semaphore_signal(barrier, inc=1, device_id={"tp": other}, device_id_type=MESH)
    pl.semaphore_wait(barrier, 2)

    acc[...] = jnp.zeros_like(acc)

    def piece_of_depth(q, carry):
        x_copy(q).wait()
        for c in first_copies(q):
            c.wait()
        deep = pl.ds(pl.multiple_of(q * chunk, chunk), chunk)
        weights = jnp.concatenate([wv[1, deep, pl.ds(0, HALF)], wv[0, deep, pl.ds(HALF, HALF)]], axis=1)
        acc[...] += jnp.dot(xv[:, deep], weights, preferred_element_type=F32)
        return carry

    lax.fori_loop(0, CHUNKS, piece_of_depth, 0)
    for at in pieces:
        pbuf[0, at] = acc[at, :HALF].astype(BF16)
        own[at] = acc[at, HALF:].astype(BF16)

    other_slab(2).start()
    p_copy(0).start()
    other_slab(1).wait()
    pbuf[1] = product(other_ref(1))

    def fence(t):
        p_copy(t - 1).wait()

        @pl.when(t >= LAG)
        def _():
            s_copy(t - LAG).wait()

        sum_chip(t - 1)
        s_copy(t - 1).start()
        p_copy(t).start()

        @pl.when(t >= LAG + 1)
        def _():
            y_copy(t - LAG - 1).start()

    def tile(t, carry):
        own_slab(t + 1).start()

        @pl.when(t + 2 < tiles)
        def _():
            other_slab(t + 2).start()

        fence(t)
        own_slab(t).wait()
        other_slab(t + 1).wait()
        both = product(wv.at[lax.rem(t, 2)])
        pbuf[lax.rem(t + 1, 2)] = both[:, :HALF]
        own[...] = both[:, HALF:]
        sum_all(t - LAG)
        return carry

    last = tiles - 1
    lax.fori_loop(1, last - 1, tile, 0)

    own_slab(last).start()
    fence(last - 1)
    own_slab(last - 1).wait()
    own[...] = product(own_ref(last - 1))
    sum_all(last - 1 - LAG)

    p_copy(last - 1).wait()
    sum_chip(last - 1)
    s_copy(last - 1).start()
    s_copy(last - 3).wait()
    y_copy(last - 4).start()
    other_slab(last).wait()
    pbuf[lax.rem(last, 2)] = product(other_ref(last))
    sum_all(last - 3)

    p_copy(last).start()
    y_copy(last - 3).start()
    own_slab(last).wait()
    own[...] = product(own_ref(last))

    p_copy(last).wait()
    sum_chip(last)
    s_copy(last).start()
    for v in (last - 2, last - 1, last):
        s_copy(v).wait()
        sum_all(v)
        y_copy(v).start()

    def finish(v, carry):
        y_copy(v).wait()
        return carry

    lax.fori_loop(0, tiles, finish, 0)


def place(y, out, sems):
    tiles = out.shape[1] // TILE
    copies = []
    for t in range(tiles):
        for h in range(2):
            copies.append(
                pltpu.make_async_copy(y.at[t + LAG, h], out.at[:, pl.ds(t * TILE + h * HALF, HALF)], sems.at[2 * t + h])
            )
    for c in copies:
        c.start()
    for c in copies:
        c.wait()


def solution(mesh):
    def local(x, w):
        rows, depth = x.shape
        columns = w.shape[1]
        tiles = columns // TILE
        x = pltpu.with_memory_space_constraint(x, pltpu.HBM)
        w = pltpu.with_memory_space_constraint(w, pltpu.HBM)
        y = pl.pallas_call(
            fused,
            out_shape=pltpu.VMEM((tiles + LAG, 2, rows, HALF), BF16),
            in_specs=[pl.BlockSpec(memory_space=pl.ANY)] * 2,
            out_specs=pl.BlockSpec(memory_space=pltpu.VMEM),
            scratch_shapes=[
                pltpu.VMEM((rows, depth), BF16),
                pltpu.VMEM((2, depth, TILE), BF16),
                pltpu.VMEM((rows, TILE), F32),
                pltpu.VMEM((rows, HALF), BF16),
                pltpu.VMEM((2, rows, HALF), BF16),
                pltpu.VMEM((2, rows, HALF), BF16),
                pltpu.VMEM((4, rows, HALF), BF16),
                pltpu.SemaphoreType.DMA((CHUNKS,)),
                pltpu.SemaphoreType.DMA((2, CHUNKS)),
                pltpu.SemaphoreType.DMA((2, 2)),
                pltpu.SemaphoreType.DMA((2,)),
                pltpu.SemaphoreType.DMA((2,)),
                pltpu.SemaphoreType.DMA((tiles,)),
                pltpu.SemaphoreType.DMA((tiles,)),
                pltpu.SemaphoreType.DMA((tiles,)),
                pltpu.SemaphoreType.DMA((tiles,)),
            ],
            compiler_params=pltpu.CompilerParams(
                collective_id=0, has_side_effects=True, vmem_limit_bytes=48 * 2**20
            ),
            name="fused",
        )(x, w)
        return pl.pallas_call(
            place,
            out_shape=jax.ShapeDtypeStruct((rows, columns), BF16),
            in_specs=[pl.BlockSpec(memory_space=pltpu.VMEM)],
            out_specs=pl.BlockSpec(memory_space=pl.ANY),
            scratch_shapes=[pltpu.SemaphoreType.DMA((2 * tiles,))],
            compiler_params=pltpu.CompilerParams(vmem_limit_bytes=16 * 2**20),
            name="place",
        )(y)

    return jax.shard_map(local, mesh=mesh, in_specs=(P("data", "tp"), P("tp", None)), out_specs=P("data", None), check_vma=False)
```

time: 371 us -> 190 us (0.51)
  Pallas kernels: 0 us -> 190 us
  waiting for transfers between devices: 178 us -> 0 us
  matrix products: 169 us -> 0 us
  between operations: 13.4 us -> 0.17 us
  local copies, waits for them, and re-layouts: 10.6 us -> 0 us
    pallas_call x0 -> x2, Pallas kernels: none -> 190 us  [the longest x1 185 us: local(): pl.pallas_call(fused, out_shape=pltpu.VMEM((tiles + LAG, 2, rows, HALF),...]
    dot_general x1 -> x0, matrix products: 169 us -> none  [local(): jnp.dot(x, w, preferred_element_type=jnp.float32).astype(jnp.bfloat16)]
    reduce_scatter x1 -> x0, waiting for transfers between devices: 95.3 us -> none  [local(): reduced = lax.psum_scatter(partial_y, 'tp', scatter_dimension=0, tiled=True)]
    all_gather x1 -> x0, waiting for transfers between devices: 82.4 us -> none  [local(): return lax.all_gather(reduced, 'tp', axis=0, tiled=True)]
    unnamed x1 -> x0, local copies, waits for them, and re-layouts: 10.6 us -> none
  transfers between devices with their start and end apart: 2 -> 0, of which waited for: 2 -> 0; matrix products, arithmetic and copies ran while one was open for 0% -> 0% of each run, Pallas kernels for 0% -> 0%
where the time goes in v2:
time: 190 us
  Pallas kernels  190 us (100%)
    pallas_call x1, Pallas kernels, local(): pl.pallas_call(fused, out_shape=pltpu.VMEM((tiles + LAG, 2, rows, HALF),...  185 us
    pallas_call x1, Pallas kernels, local(): pl.pallas_call(place, out_shape=jax.ShapeDtypeStruct((rows, columns), BF1...  4.94 us

profile of v2, /device:TPU:0, one launch (start us, length us, event | category | flops | bytes accessed | tf_op | source)
XLA Modules:
  0.0 190.2 jit_solution(1433896344882074633)
XLA Ops:
  0.0 185.1 %fused.1.y = bf16[27,2,512,256]{3,2,1,0:T(8,128)(2,1)S(1)} custom-call(bf16[512,12288]{1,0:T(8,128)(2,1)} %x.1, bf16[12288,12288]{1,0:T(8,128)(2,1)} %w.1), custom_call_target="tpu_custom_call" | custom-call | tf_op jit(solution)/shard_map/fused/pallas_call | solution.py:208
  185.1 4.9 %place.1 = bf16[512,12288]{1,0:T(8,128)(2,1)} custom-call(bf16[27,2,512,256]{3,2,1,0:T(8,128)(2,1)S(1)} %fused.1.y), custom_call_target="tpu_custom_call" | custom-call | tf_op jit(solution)/shard_map/place/pallas_call | solution.py:236

commit v3 on v2

--- a/solution.py
+++ b/solution.py
@@ -12,6 +12,8 @@
 TILE = 2 * HALF
 CHUNKS = 8
 PIECE = 128
+AHEAD = 3
+SPLIT = 4
 LAG = 3
 
 
@@ -19,7 +21,11 @@
     depth = x.shape[1]
     tiles = w.shape[1] // TILE
     chunk = depth // CHUNKS
-    pieces = [pl.ds(r, PIECE) for r in range(0, x.shape[0], PIECE)]
+    rows = x.shape[0]
+    middle, shallow = rows // 2, depth // 2
+    last = tiles - 1
+    pieces = [pl.ds(r, PIECE) for r in range(0, rows, PIECE)]
+    half_rows = [pl.ds(0, middle), pl.ds(middle, middle)]
     me = lax.axis_index("tp")
     core = lax.rem(me, 2)
     partner = me + 1 - 2 * core
@@ -58,12 +64,17 @@
             device_id={"tp": partner}, device_id_type=MESH,
         )
 
-    def s_copy(v):
+    def s_copy(v, h):
         s = lax.rem(v, 4)
         return pltpu.make_async_remote_copy(
-            src_ref=sbuf.at[s], dst_ref=y.at[v + LAG, core], send_sem=s_send.at[v], recv_sem=s_recv.at[v],
+            src_ref=sbuf.at[s, half_rows[h]], dst_ref=y.at[v + LAG, core, half_rows[h]],
+            send_sem=s_send.at[v, h], recv_sem=s_recv.at[v, h],
             device_id={"tp": across}, device_id_type=MESH,
         )
+
+    def s_wait(v):
+        for h in range(2):
+            s_copy(v, h).wait()
 
     def y_copy(v):
         return pltpu.make_async_remote_copy(
@@ -71,23 +82,46 @@
             device_id={"tp": partner}, device_id_type=MESH,
         )
 
-    def sum_chip(v):
-        for at in pieces:
+    def y_last(h):
+        return pltpu.make_async_remote_copy(
+            src_ref=y.at[last + LAG, core, half_rows[h]], dst_ref=y.at[last + LAG, core, half_rows[h]],
+            send_sem=y_send.at[last + h], recv_sem=y_recv.at[last + h],
+            device_id={"tp": partner}, device_id_type=MESH,
+        )
+
+    def send_chip(v, h):
+        for at in pieces[h * len(pieces) // 2 : (h + 1) * len(pieces) // 2]:
             sbuf[lax.rem(v, 4), at] = own[at] + precv[lax.rem(v, 2), at]
-
-    def sum_all(v):
-        for at in pieces:
+        s_copy(v, h).start()
+
+    def sum_all(v, which=pieces):
+        for at in which:
             y[v + LAG, core, at] = sbuf[lax.rem(v + 4, 4), at] + y[v + LAG, core, at]
 
-    def product(weights):
-        return jnp.dot(xv[...], weights[...], preferred_element_type=F32).astype(BF16)
-
-    for q in range(CHUNKS):
+    def dot(a, b):
+        return jnp.dot(a, b, preferred_element_type=F32)
+
+    def other_product(t):
+        weights = other_ref(t)[...]
+        slot = lax.rem(t, 2)
+        halves = [dot(xv[at], weights).astype(BF16) for at in half_rows]
+        for at, half in zip(half_rows, halves):
+            pbuf[slot, at] = half
+
+    def own_product(t, h):
+        near, far = pl.ds(0, shallow), pl.ds(shallow, shallow)
+        cols = pl.ds(HALF, HALF)
+        first = dot(xv[half_rows[h], near], wv[lax.rem(t, 2), near, cols])
+        second = dot(xv[half_rows[h], far], wv[lax.rem(t, 2), far, cols])
+        own[half_rows[h]] = (first + second).astype(BF16)
+
+    def first_start(q):
         x_copy(q).start()
         for c in first_copies(q):
             c.start()
-    other_slab(1).start()
-    own_slab(1).start()
+
+    for q in range(AHEAD):
+        first_start(q)
 
     barrier = pltpu.get_barrier_semaphore()
     for other in (partner, across):
@@ -100,6 +134,19 @@
         x_copy(q).wait()
         for c in first_copies(q):
             c.wait()
+
+        @pl.when(q + AHEAD < CHUNKS)
+        def _():
+            first_start(q + AHEAD)
+
+        @pl.when(q == CHUNKS - AHEAD)
+        def _():
+            other_slab(1).start()
+
+        @pl.when(q == CHUNKS - 1)
+        def _():
+            own_slab(1).start()
+
         deep = pl.ds(pl.multiple_of(q * chunk, chunk), chunk)
         weights = jnp.concatenate([wv[1, deep, pl.ds(0, HALF)], wv[0, deep, pl.ds(HALF, HALF)]], axis=1)
         acc[...] += jnp.dot(xv[:, deep], weights, preferred_element_type=F32)
@@ -113,75 +160,82 @@
     other_slab(2).start()
     p_copy(0).start()
     other_slab(1).wait()
-    pbuf[1] = product(other_ref(1))
+    other_product(1)
 
     def fence(t):
         p_copy(t - 1).wait()
 
         @pl.when(t >= LAG)
         def _():
-            s_copy(t - LAG).wait()
-
-        sum_chip(t - 1)
-        s_copy(t - 1).start()
+            s_wait(t - LAG)
+
+        send_chip(t - 1, 0)
+        send_chip(t - 1, 1)
         p_copy(t).start()
 
         @pl.when(t >= LAG + 1)
         def _():
             y_copy(t - LAG - 1).start()
 
+    def next_slabs(t):
+        own_slab(t + 1).start()
+
+        @pl.when(t + 2 < tiles)
+        def _():
+            other_slab(t + 2).start()
+
     def tile(t, carry):
-        own_slab(t + 1).start()
-
-        @pl.when(t + 2 < tiles)
-        def _():
-            other_slab(t + 2).start()
-
+        next_slabs(t)
         fence(t)
         own_slab(t).wait()
         other_slab(t + 1).wait()
-        both = product(wv.at[lax.rem(t, 2)])
+        both = dot(xv[...], wv[lax.rem(t, 2)]).astype(BF16)
         pbuf[lax.rem(t + 1, 2)] = both[:, :HALF]
         own[...] = both[:, HALF:]
         sum_all(t - LAG)
         return carry
 
-    last = tiles - 1
-    lax.fori_loop(1, last - 1, tile, 0)
-
-    own_slab(last).start()
-    fence(last - 1)
-    own_slab(last - 1).wait()
-    own[...] = product(own_ref(last - 1))
-    sum_all(last - 1 - LAG)
-
-    p_copy(last - 1).wait()
-    sum_chip(last - 1)
-    s_copy(last - 1).start()
-    s_copy(last - 3).wait()
-    y_copy(last - 4).start()
-    other_slab(last).wait()
-    pbuf[lax.rem(last, 2)] = product(other_ref(last))
-    sum_all(last - 3)
-
-    p_copy(last).start()
-    y_copy(last - 3).start()
-    own_slab(last).wait()
-    own[...] = product(own_ref(last))
-
-    p_copy(last).wait()
-    sum_chip(last)
-    s_copy(last).start()
-    for v in (last - 2, last - 1, last):
-        s_copy(v).wait()
+    def own_halves(t):
+        own_slab(t).wait()
+        own_product(t, 0)
+        sum_all(t - LAG)
+        p_copy(t).wait()
+        send_chip(t, 0)
+        own_product(t, 1)
+        send_chip(t, 1)
+
+    def split_tile(t, carry):
+        next_slabs(t)
+        own_halves(t)
+        s_wait(t - 2)
+        other_slab(t + 1).wait()
+        other_product(t + 1)
+        p_copy(t + 1).start()
+        y_copy(t - LAG).start()
+        return carry
+
+    lax.fori_loop(1, tiles - SPLIT, tile, 0)
+    fence(tiles - SPLIT)
+    lax.fori_loop(tiles - SPLIT, last, split_tile, 0)
+    own_halves(last)
+
+    y_copy(last - LAG).start()
+    for v in (last - 2, last - 1):
+        s_wait(v)
         sum_all(v)
         y_copy(v).start()
+    for h in range(2):
+        s_copy(last, h).wait()
+        sum_all(last, pieces[h * len(pieces) // 2 : (h + 1) * len(pieces) // 2])
+        y_last(h).start()
 
     def finish(v, carry):
         y_copy(v).wait()
         return carry
 
-    lax.fori_loop(0, tiles, finish, 0)
+    lax.fori_loop(0, last, finish, 0)
+    for h in range(2):
+        y_last(h).wait()
 
 
 def place(y, out, sems):
@@ -223,10 +277,10 @@
                 pltpu.SemaphoreType.DMA((2, 2)),
                 pltpu.SemaphoreType.DMA((2,)),
                 pltpu.SemaphoreType.DMA((2,)),
-                pltpu.SemaphoreType.DMA((tiles,)),
-                pltpu.SemaphoreType.DMA((tiles,)),
-                pltpu.SemaphoreType.DMA((tiles,)),
-                pltpu.SemaphoreType.DMA((tiles,)),
+                pltpu.SemaphoreType.DMA((tiles, 2)),
+                pltpu.SemaphoreType.DMA((tiles, 2)),
+                pltpu.SemaphoreType.DMA((tiles + 1,)),
+                pltpu.SemaphoreType.DMA((tiles + 1,)),
             ],
             compiler_params=pltpu.CompilerParams(
                 collective_id=0, has_side_effects=True, vmem_limit_bytes=48 * 2**20

time: 190 us -> 194 us (1.021)
  Pallas kernels: 190 us -> 194 us
    pallas_call x1, Pallas kernels: 185 us -> 189 us  [local(): pl.pallas_call(fused, out_shape=pltpu.VMEM((tiles + LAG, 2, rows, HALF),...]
where the time goes in v3:
time: 194 us
  Pallas kernels  194 us (100%)
    pallas_call x1, Pallas kernels, local(): pl.pallas_call(fused, out_shape=pltpu.VMEM((tiles + LAG, 2, rows, HALF),...  189 us
    pallas_call x1, Pallas kernels, local(): pl.pallas_call(place, out_shape=jax.ShapeDtypeStruct((rows, columns), BF1...  4.94 us

profile of v3, /device:TPU:0, one launch (start us, length us, event | category | flops | bytes accessed | tf_op | source)
XLA Modules:
  0.0 194.0 jit_solution(878049764033848474)
XLA Ops:
  0.0 188.8 %fused.1.y = bf16[27,2,512,256]{3,2,1,0:T(8,128)(2,1)S(1)} custom-call(bf16[512,12288]{1,0:T(8,128)(2,1)} %x.1, bf16[12288,12288]{1,0:T(8,128)(2,1)} %w.1), custom_call_target="tpu_custom_call" | custom-call | tf_op jit(solution)/shard_map/fused/pallas_call | solution.py:262
  188.9 4.9 %place.1 = bf16[512,12288]{1,0:T(8,128)(2,1)} custom-call(bf16[27,2,512,256]{3,2,1,0:T(8,128)(2,1)S(1)} %fused.1.y), custom_call_target="tpu_custom_call" | custom-call | tf_op jit(solution)/shard_map/place/pallas_call | solution.py:290

commit v4 on v3

--- a/solution.py
+++ b/solution.py
@@ -111,9 +111,10 @@
     def own_product(t, h):
         near, far = pl.ds(0, shallow), pl.ds(shallow, shallow)
         cols = pl.ds(HALF, HALF)
-        first = dot(xv[half_rows[h], near], wv[lax.rem(t, 2), near, cols])
-        second = dot(xv[half_rows[h], far], wv[lax.rem(t, 2), far, cols])
-        own[half_rows[h]] = (first + second).astype(BF16)
+        weights = wv.at[lax.rem(t, 2), :, cols]
+        acc[half_rows[h], :HALF] = dot(xv[half_rows[h], near], weights[near])
+        second = dot(xv[half_rows[h], far], weights[far])
+        own[half_rows[h]] = (acc[half_rows[h], :HALF] + second).astype(BF16)
 
     def first_start(q):
         x_copy(q).start()

time: 194 us -> 182 us (0.938)
  Pallas kernels: 194 us -> 182 us
    pallas_call x1, Pallas kernels: 189 us -> 177 us  [local(): pl.pallas_call(fused, out_shape=pltpu.VMEM((tiles + LAG, 2, rows, HALF),...]
where the time goes in v4:
time: 182 us
  Pallas kernels  182 us (100%)
    pallas_call x1, Pallas kernels, local(): pl.pallas_call(fused, out_shape=pltpu.VMEM((tiles + LAG, 2, rows, HALF),...  177 us
    pallas_call x1, Pallas kernels, local(): pl.pallas_call(place, out_shape=jax.ShapeDtypeStruct((rows, columns), BF1...  4.94 us

profile of v4, /device:TPU:0, one launch (start us, length us, event | category | flops | bytes accessed | tf_op | source)
XLA Modules:
  0.0 182.2 jit_solution(4320440951464119082)
XLA Ops:
  0.0 177.1 %fused.1.y = bf16[27,2,512,256]{3,2,1,0:T(8,128)(2,1)S(1)} custom-call(bf16[512,12288]{1,0:T(8,128)(2,1)} %x.1, bf16[12288,12288]{1,0:T(8,128)(2,1)} %w.1), custom_call_target="tpu_custom_call" | custom-call | tf_op jit(solution)/shard_map/fused/pallas_call | solution.py:263
  177.1 4.9 %place.1 = bf16[512,12288]{1,0:T(8,128)(2,1)} custom-call(bf16[27,2,512,256]{3,2,1,0:T(8,128)(2,1)S(1)} %fused.1.y), custom_call_target="tpu_custom_call" | custom-call | tf_op jit(solution)/shard_map/place/pallas_call | solution.py:291

commit v5 on v4

--- a/solution.py
+++ b/solution.py
@@ -12,8 +12,8 @@
 TILE = 2 * HALF
 CHUNKS = 8
 PIECE = 128
-AHEAD = 3
-SPLIT = 4
+AHEAD = 4
+SPLIT = 5
 LAG = 3
 
 

time: 182 us -> 183 us (level)
  no operation moved by 1% of the time
where the time goes in v5:
time: 183 us
  Pallas kernels  182 us (99%)
    pallas_call x1, Pallas kernels, local(): pl.pallas_call(fused, out_shape=pltpu.VMEM((tiles + LAG, 2, rows, HALF),...  177 us
    pallas_call x1, Pallas kernels, local(): pl.pallas_call(place, out_shape=jax.ShapeDtypeStruct((rows, columns), BF1...  4.94 us

profile of v5, /device:TPU:0, one launch (start us, length us, event | category | flops | bytes accessed | tf_op | source)
XLA Modules:
  0.0 182.6 jit_solution(10583846316685971713)
XLA Ops:
  0.0 177.5 %fused.1.y = bf16[27,2,512,256]{3,2,1,0:T(8,128)(2,1)S(1)} custom-call(bf16[512,12288]{1,0:T(8,128)(2,1)} %x.1, bf16[12288,12288]{1,0:T(8,128)(2,1)} %w.1), custom_call_target="tpu_custom_call" | custom-call | tf_op jit(solution)/shard_map/fused/pallas_call | solution.py:263
  177.5 4.9 %place.1 = bf16[512,12288]{1,0:T(8,128)(2,1)} custom-call(bf16[27,2,512,256]{3,2,1,0:T(8,128)(2,1)S(1)} %fused.1.y), custom_call_target="tpu_custom_call" | custom-call | tf_op jit(solution)/shard_map/place/pallas_call | solution.py:291
